TPU v7x, 32 devices: a whole 2x2x4 slice. The times are simulated.
32 devices in a mesh: row: 8 (over z, core), col: 4 (over y, x).
Axes of the slice: x: 2, y: 2, z: 4, core: 2. Of those that a mesh axis runs over, the one named last changes fastest.
Arguments:
- ancestor_inverse: float32 [12288, 12288], P('row', 'col'), may hold values from -6 to 6
- panel: float32 [5632, 512], P('col', 'row'), may hold values from -0.078125 to 0.078125
- unit_inverse: float32 [512, 512], P('row'), may hold values from -1 to 1, as said below
- pivot_inverse: float32 [512, 512], P('row', 'col'), may hold values from -6 to 6
- panel_blocks: int32 [44], replicated, may hold values from 0 to 95, as said below
Outputs:
- inverse_row: float32 [512, 12288], P('col', 'row')
- diagonal_block: float32 [512, 512], P('row', 'col')
Inputs may be any that keep to these rules, and one draw needn't show every extreme that they name: `panel_blocks`: Distinct, in no particular order. Among the window blocks c * 24 to c * 24 + 23 of any process column c at most 12 are listed, and exactly 12 for some columns. `unit_inverse`: unit lower triangular: ones on the diagonal, zeros above it.
All inputs are finite; a program needn't handle non-finite values.
Results may differ from a plain program's by a relative error of at most 0.00011.
Values sent between devices are 32-bit elements; how exact they have to be, the bound alone decides.
A program may use at most 128 MiB of HBM per device.

v0:
```python
import jax
import jax.numpy as jnp
from jax import lax
from jax.sharding import PartitionSpec as P

BLK = 128


def broadcast(value, axis, root):
    mine = lax.axis_index(axis) == root
    return lax.psum(jnp.where(mine, value, jnp.zeros_like(value)), axis)


def place_blocks(stacked, block_ids, wanted):
    onehot = (block_ids[None, :] == wanted[:, None]).astype(jnp.float32)
    placed = jnp.einsum("kp,pbw->kbw", onehot, stacked, precision=lax.Precision.HIGHEST)
    return placed.reshape(wanted.shape[0] * stacked.shape[1], stacked.shape[2])


def on_device(ancestor_inverse, panel, unit_inverse, pivot_inverse, panel_blocks):
    highest = lax.Precision.HIGHEST
    row_index = lax.axis_index("row")
    col_index = lax.axis_index("col")
    rows_here, cols_here = ancestor_inverse.shape
    width = unit_inverse.shape[1]
    block_total = panel_blocks.shape[0]
    range_blocks = cols_here // BLK
    row_blocks = rows_here // BLK
    first_block = col_index * range_blocks
    partial_value = jnp.dot(
        panel, unit_inverse, precision=highest, preferred_element_type=jnp.float32
    )
    normal = lax.psum_scatter(partial_value, "row", scatter_dimension=1, tiled=True)
    all_rows = lax.all_gather(normal, "col", axis=0, tiled=True)
    stacked = all_rows.reshape(block_total, BLK, all_rows.shape[1])
    slot_count = range_blocks // 2
    in_range = ((panel_blocks >= first_block) & (panel_blocks < first_block + range_blocks)).astype(
        jnp.int32
    )
    rank_of = jnp.cumsum(in_range) - 1
    slot_ids = jnp.arange(slot_count, dtype=jnp.int32)
    selected = (in_range[None, :] == 1) & (rank_of[None, :] == slot_ids[:, None])
    chosen = jnp.einsum("sp,pbw->sbw", selected.astype(jnp.float32), stacked, precision=highest)
    chosen = chosen.reshape(slot_count * BLK, stacked.shape[2])
    chosen_ids = jnp.sum(jnp.where(selected, panel_blocks[None, :], 0), axis=1)
    slot_live = jnp.sum(selected.astype(jnp.int32), axis=1) > 0
    window_ids = jnp.where(slot_live, chosen_ids, -1)
    local_ids = jnp.clip(chosen_ids - first_block, 0, range_blocks - 1)
    window = lax.all_gather(chosen, "row", axis=1, tiled=True)
    columns = jnp.take(ancestor_inverse.reshape(rows_here, range_blocks, BLK), local_ids, axis=1)
    columns = columns.reshape(rows_here, slot_count * BLK)
    inverse_tile = lax.psum_scatter(
        -lax.dot_general(
            window,
            columns,
            (((0,), (1,)), ((), ())),
            precision=highest,
            preferred_element_type=jnp.float32,
        ),
        "col",
        scatter_dimension=0,
        tiled=True,
    )
    row_ids = row_index * row_blocks + jnp.arange(row_blocks, dtype=jnp.int32)
    window_stack = window.reshape(window.shape[0] // BLK, BLK, width)
    candidate = place_blocks(window_stack, window_ids, row_ids)
    owner = row_index * rows_here // cols_here
    own_window = broadcast(candidate, "col", owner)
    crossed = -lax.dot_general(
        own_window,
        inverse_tile,
        (((0,), (1,)), ((), ())),
        precision=highest,
        preferred_element_type=jnp.float32,
    )
    diagonal_block = pivot_inverse + lax.psum_scatter(
        crossed, "row", scatter_dimension=0, tiled=True
    )
    return (inverse_tile, diagonal_block)


def solution(mesh):
    return jax.shard_map(
        on_device,
        mesh=mesh,
        in_specs=(P("row", "col"), P("col", "row"), P("row", None), P("row", "col"), P()),
        out_specs=(P("col", "row"), P("row", "col")),
        check_vma=False,
    )
```

profile of v0, /device:TPU:0, one launch (start us, length us, event | category | flops | bytes accessed | tf_op | source)
XLA Modules:
  0.0 318.0 jit_solution(3767256040483934672)
XLA Ops:
  7.2 0.0 copy-start
  7.2 0.0 copy-start.4
  7.2 0.0 reduce-scatter.4.cloned.1.call-start
  7.2 0.9 copy-done
  8.2 4.9 %fusion.16 = f32[1408,512]{0,1:T(8,128)} fusion(f32[1408,64]{0,1:T(8,128)S(1)} %copy-done, f32[64,512]{1,0:T(8,128)} %param.7), kind=kOutput, calls=%fused_computation.32 | convolution fusion | flops 553648128 | bytes 3375104 | tf_op jit(solution)/shard_map/dot_general | solution.py:30
  13.1 0.0 reduce-scatter.4.cloned.1.call-update
  13.1 0.0 all-gather.3.cloned.1.call-start
  13.2 41.8 %reduce-scatter.4.cloned.1.call-done = f32[1408,64]{0,1:T(8,128)} async-done(((f32[1408,512]{0,1:T(8,128)}), f32[1408,64]{0,1:T(8,128)}) %reduce-scatter.4.cloned.1.call-update) | async-done | bytes 360464 | tf_op jit(solution)/shard_map/reduce_scatter | solution.py:33
  54.9 0.0 all-gather.3.cloned.1.call-update
  55.0 0.0 all-gather.5.cloned.1.call-start
  55.0 0.0 copy-done.4
  55.0 0.1 copy.13
  55.1 0.1 reduce-window.8
  55.2 0.1 add_reduce_fusion
  55.3 30.5 %all-gather.3.cloned.1.call-done = f32[5632,64]{0,1:T(8,128)} async-done(((f32[1408,64]{0,1:T(8,128)}), f32[5632,64]{0,1:T(8,128)}) %all-gather.3.cloned.1.call-update) | async-done | bytes 1441808 | tf_op jit(solution)/shard_map/all_gather | solution.py:34
  85.8 1.5 reshape.93
  87.3 0.6 fusion.7
  87.9 0.9 copy.26
  88.8 0.0 all-gather.5.cloned.1.call-update
  88.8 0.0 all-reduce.2.cloned.1.call-start
  88.9 18.8 %copy.14 = f32[1536,3072]{0,1:T(8,128)} copy(f32[1536,3072]{1,0:T(8,128)} %param.5) | data formatting | bytes 37748736 | tf_op args[0]
  107.7 18.7 %copy.15 = f32[1536,24,128]{2,0,1:T(8,128)} copy(f32[1536,24,128]{0,2,1:T(8,128)} %bitcast.34) | data formatting | bytes 37748736 | tf_op jit(solution)/shard_map/reshape | solution.py:50
  126.4 0.1 convert_reduce_fusion
  126.5 0.6 all-gather.5.cloned.1.call-done
  127.2 2.4 copy.17
  129.6 4.0 %fusion.2 = f32[12,128,512]{2,0,1:T(8,128)S(1)} fusion(f32[12,128,512]{2,1,0:T(8,128)S(1)} %bitcast.36, pred[]{:T(512)S(6)} %eq.41, s32[12]{0:T(128)S(1)} %get-tuple-element.6, s32[12]{0:T(128)S(1)} %get-tuple-element.7), kind=kOutput, calls=%fused_computation.5 | convolution fusion | flops 114032784 | bytes 6291553 | tf_op jit(solution)/shard_map/kp,pbw->kbw/dot_general | solution.py:16
  133.6 3.5 %copy.19 = f32[12,128,512]{2,1,0:T(8,128)} copy(f32[12,128,512]{2,0,1:T(8,128)S(1)} %fusion.2) | data formatting | bytes 6291456 | tf_op jit(solution)/shard_map/jit(_where)/select_n | solution.py:11
  137.1 0.0 all-reduce.2.cloned.1.call-update
  137.1 0.0 reduce-scatter.6.cloned.1.call-start
  137.2 12.3 %gather_fusion = f32[12,1536,128]{2,1,0:T(8,128)} fusion(f32[1536,24,128]{2,0,1:T(8,128)} %copy.15, s32[1024]{0:T(1024)S(1)} %pad_clamp_fusion), kind=kCustom, calls=%fused_computation | custom fusion | bytes 18874416 | tf_op jit(solution)/shard_map/jit(_take)/gather | solution.py:50
  149.5 9.8 %copy.16 = f32[1536,12,128]{0,2,1:T(8,128)} copy(f32[1536,12,128]{2,0,1:T(8,128)} %bitcast.35) | data formatting | bytes 18874368 | tf_op jit(solution)/shard_map/jit(_take)/gather | solution.py:50
  159.2 0.1 broadcast_bitcast_fusion
  159.3 0.0 copy-start.2
  159.3 4.6 %bitcast_select_fusion = f32[1536,1536]{0,1:T(8,128)S(1)} fusion(f32[1536,12,128]{0,2,1:T(8,128)} %copy.16, pred[1536]{0:T(1024)(128)(4,1)S(1)} %broadcast_bitcast_fusion), kind=kLoop, calls=%fused_computation.1 | loop fusion | flops 2359296 | bytes 18875904 | tf_op jit(solution)/shard_map/jit(_take)/select_n | solution.py:50
  164.0 0.1 copy-done.2
  164.0 17.1 %convolution_negate_fusion = f32[512,1536]{1,0:T(8,128)} fusion(f32[1536,512]{0,1:T(8,128)S(1)} %copy-done.2, f32[1536,1536]{0,1:T(8,128)S(1)} %bitcast_select_fusion), kind=kOutput, calls=%fused_computation.4 | convolution fusion | flops 14496301056 | bytes 15728640 | tf_op jit(solution)/shard_map/dot_general | solution.py:53
  181.1 0.0 copy-start.1
  181.1 0.0 copy-start.3
  181.1 0.0 reduce-scatter.6.cloned.1.call-update
  181.1 0.0 reduce-scatter.8.cloned.1.call-start
  181.2 42.4 %all-reduce.2.cloned.1.call-done = f32[1536,512]{1,0:T(8,128)} async-done(((f32[1536,512]{1,0:T(8,128)}), f32[1536,512]{1,0:T(8,128)}) %all-reduce.2.cloned.1.call-update) | async-done | bytes 3145744 | tf_op jit(solution)/shard_map/psum | solution.py:11
  223.6 47.3 %reduce-scatter.6.cloned.1.call-done = f32[128,1536]{1,0:T(8,128)} async-done(((f32[512,1536]{1,0:T(8,128)}), f32[128,1536]{1,0:T(8,128)}) %reduce-scatter.6.cloned.1.call-update) | async-done | bytes 786448 | tf_op jit(solution)/shard_map/reduce_scatter | solution.py:52
  270.9 7.8 %convolution_negate_fusion.1 = f32[512,128]{1,0:T(8,128)} fusion(f32[1536,512]{1,0:T(8,128)} %all-reduce.2.cloned.1.call-done, f32[128,1536]{1,0:T(8,128)} %reduce-scatter.6.cloned.1.call-done), kind=kOutput, calls=%fused_computation.6 | convolution fusion | flops 1208025088 | bytes 4194304 | tf_op jit(solution)/shard_map/dot_general | solution.py:69
  278.8 0.0 reduce-scatter.8.cloned.1.call-update
  278.8 31.0 %reduce-scatter.8.cloned.1.call-done = f32[64,128]{1,0:T(8,128)} async-done(((f32[512,128]{1,0:T(8,128)}), f32[64,128]{1,0:T(8,128)}) %reduce-scatter.8.cloned.1.call-update) | async-done | bytes 32784 | tf_op jit(solution)/shard_map/reduce_scatter | solution.py:76
  309.8 0.0 copy-done.3
  309.8 1.4 add.51
  311.1 0.0 copy-done.1
  (5 shorter events, 0.0 us)
Async XLA Ops:
  7.2 1.0 copy-start
  7.2 47.8 %copy-start.4 = (s32[44]{0:T(128)S(1)}, s32[44]{0:T(128)}, u32[]{:S(2)}) copy-start(s32[44]{0:T(128)} %param.9) | copy-start | bytes 532
  7.2 47.8 %reduce-scatter.4.cloned.1.call-start = ((), (), s32[]{:S(2)}) async-start(), calls=%async_computation.3 | async-start | bytes 3244032 | tf_op jit(solution)/shard_map/reduce_scatter | solution.py:33
  13.1 72.7 %all-gather.3.cloned.1.call-start = ((), (), s32[]{:S(2)}) async-start(), calls=%async_computation.4 | async-start | bytes 1802240 | tf_op jit(solution)/shard_map/all_gather | solution.py:34
  55.0 72.2 %all-gather.5.cloned.1.call-start = ((), (), s32[]{:S(2)}) async-start(), calls=%async_computation.5 | async-start | bytes 3538944 | tf_op jit(solution)/shard_map/all_gather | solution.py:49
  88.8 134.8 %all-reduce.2.cloned.1.call-start = ((), (), s32[]{:S(2)}) async-start(), calls=%async_computation.7 | async-start | bytes 6291456 | tf_op jit(solution)/shard_map/psum | solution.py:11
  137.1 133.8 %reduce-scatter.6.cloned.1.call-start = ((), (), s32[]{:S(2)}) async-start(), calls=%async_computation.6 | async-start | bytes 3932160 | tf_op jit(solution)/shard_map/reduce_scatter | solution.py:52
  159.3 4.7 %copy-start.2 = (f32[1536,512]{0,1:T(8,128)S(1)}, f32[1536,512]{0,1:T(8,128)}, u32[]{:S(2)}) copy-start(f32[1536,512]{0,1:T(8,128)} %all-gather.5.cloned.1.call-done) | copy-start | bytes 9437188
  181.1 130.0 %copy-start.1 = (f32[1408,64]{0,1:T(8,128)S(1)}, f32[1408,64]{0,1:T(8,128)}, u32[]{:S(2)}) copy-start(f32[1408,64]{0,1:T(8,128)} %param.6) | copy-start | bytes 1081348
  181.1 128.7 %copy-start.3 = (f32[64,128]{1,0:T(8,128)S(1)}, f32[64,128]{1,0:T(8,128)}, u32[]{:S(2)}) copy-start(f32[64,128]{1,0:T(8,128)} %param.8) | copy-start | bytes 98308
  181.1 128.6 %reduce-scatter.8.cloned.1.call-start = ((), (), s32[]{:S(2)}) async-start(), calls=%async_computation.8 | async-start | bytes 294912 | tf_op jit(solution)/shard_map/reduce_scatter | solution.py:76
Sparse Core Ops, SparseCore 0:
  13.2 41.6 reduce-scatter.3
  56.8 28.9 all-gather.2
  88.9 38.2 all-gather.4
  137.2 86.3 all-reduce.1
  227.0 43.8 reduce-scatter.5
  278.9 30.8 reduce-scatter.7
where the time goes:
time: 319 us; the launch traced here: 318 us
  waiting for transfers between devices  194 us (61%)
  local copies, waits for them, and re-layouts  68.9 us (22%)
  matrix products  34.5 us (11%)
  between operations  14.2 us (4%)
  other arithmetic  6.36 us (2%)
    reduce_scatter x1, waiting for transfers between devices, on_device(): lax.psum_scatter(-lax.dot_general(window, columns, (((0,), (1,)), ((), ()...  47.3 us
    psum x1, waiting for transfers between devices, broadcast(): return lax.psum(jnp.where(mine, value, jnp.zeros_like(value)), axis)  42.4 us
    reduce_scatter x1, waiting for transfers between devices, on_device(): lax.psum_scatter(partial_value, 'row', scatter_dimension=1, tiled=True)  41.8 us
    reduce_scatter x1, waiting for transfers between devices, on_device(): lax.psum_scatter(crossed, 'row', scatter_dimension=0, tiled=True)  31 us
    all_gather x1, waiting for transfers between devices, on_device(): all_rows = lax.all_gather(normal, 'col', axis=0, tiled=True)  30.5 us
    gather x2, local copies, waits for them, and re-layouts, on_device(): jnp.take(ancestor_inverse.reshape(rows_here, range_blocks, BLK), local_id...  22 us
    unnamed x12, local copies, waits for them, and re-layouts  20.7 us
    reshape x1, local copies, waits for them, and re-layouts, on_device(): ancestor_inverse.reshape(rows_here, range_blocks, BLK)  18.7 us
  transfers between devices with their start and end apart: 6, of which 6 were waited for; matrix products, arithmetic and copies ran while one was open for 26% of the time, Pallas kernels for 0%

commit v1 on v0

--- a/solution.py
+++ b/solution.py
@@ -8,7 +8,7 @@
 
 def broadcast(value, axis, root):
     mine = lax.axis_index(axis) == root
-    return lax.psum(jnp.where(mine, value, jnp.zeros_like(value)), axis)
+    return jnp.sum(lax.all_gather(jnp.where(mine, value, jnp.zeros_like(value)), axis), axis=0)
 
 
 def place_blocks(stacked, block_ids, wanted):

time: 319 us -> 353 us (1.11)
  waiting for transfers between devices: 194 us -> 223 us
  other arithmetic: 6.36 us -> 12.8 us
    psum x1 -> x0, waiting for transfers between devices: 42.4 us -> none  [broadcast(): return lax.psum(jnp.where(mine, value, jnp.zeros_like(value)), axis)]
    all_gather x0 -> x1, waiting for transfers between devices: none -> 40.5 us  [broadcast(): lax.all_gather(jnp.where(mine, value, jnp.zeros_like(value)), axis)]
    all_gather x1, waiting for transfers between devices: 0.65 us -> 38.2 us  [on_device(): window = lax.all_gather(chosen, 'row', axis=1, tiled=True)]
    reduce_scatter x1, waiting for transfers between devices: 47.3 us -> 40.8 us  [on_device(): lax.psum_scatter(-lax.dot_general(window, columns, (((0,), (1,)), ((), ()...]
    reduce_sum x0 -> x1, other arithmetic: none -> 6.51 us  [broadcast(): jnp.sum(lax.all_gather(jnp.where(mine, value, jnp.zeros_like(value)), axi...]
  transfers between devices with their start and end apart: 6 -> 6, of which waited for: 6 -> 6; matrix products, arithmetic and copies ran while one was open for 26% -> 25% of each run, Pallas kernels for 0% -> 0%
where the time goes in v1:
time: 353 us; the launch traced here: 352 us
  waiting for transfers between devices  223 us (63%)
  local copies, waits for them, and re-layouts  68.4 us (19%)
  matrix products  33.5 us (9%)
  between operations  14.2 us (4%)
  other arithmetic  12.8 us (4%)
    reduce_scatter x1, waiting for transfers between devices, on_device(): lax.psum_scatter(partial_value, 'row', scatter_dimension=1, tiled=True)  41.8 us
    reduce_scatter x1, waiting for transfers between devices, on_device(): lax.psum_scatter(-lax.dot_general(window, columns, (((0,), (1,)), ((), ()...  40.8 us
    all_gather x1, waiting for transfers between devices, broadcast(): lax.all_gather(jnp.where(mine, value, jnp.zeros_like(value)), axis)  40.5 us
    all_gather x1, waiting for transfers between devices, on_device(): window = lax.all_gather(chosen, 'row', axis=1, tiled=True)  38.2 us
    reduce_scatter x1, waiting for transfers between devices, on_device(): lax.psum_scatter(crossed, 'row', scatter_dimension=0, tiled=True)  31 us
    all_gather x1, waiting for transfers between devices, on_device(): all_rows = lax.all_gather(normal, 'col', axis=0, tiled=True)  30.5 us
    gather x2, local copies, waits for them, and re-layouts, on_device(): jnp.take(ancestor_inverse.reshape(rows_here, range_blocks, BLK), local_id...  21.2 us
    unnamed x12, local copies, waits for them, and re-layouts  21.1 us
  transfers between devices with their start and end apart: 6, of which 6 were waited for; matrix products, arithmetic and copies ran while one was open for 25% of the time, Pallas kernels for 0%

profile of v1, /device:TPU:0, one launch (start us, length us, event | category | flops | bytes accessed | tf_op | source)
XLA Modules:
  0.0 352.0 jit_solution(10050021816249401080)
XLA Ops:
  7.2 0.0 copy-start
  7.2 0.0 copy-start.4
  7.2 0.0 reduce-scatter.4.cloned.1.call-start
  7.2 0.9 copy-done
  8.2 4.9 %fusion.16 = f32[1408,512]{0,1:T(8,128)} fusion(f32[1408,64]{0,1:T(8,128)S(1)} %copy-done, f32[64,512]{1,0:T(8,128)} %param.7), kind=kOutput, calls=%fused_computation.32 | convolution fusion | flops 553648128 | bytes 3375104 | tf_op jit(solution)/shard_map/dot_general | solution.py:30
  13.1 0.0 reduce-scatter.4.cloned.1.call-update
  13.1 0.0 all-gather.4.cloned.1.call-start
  13.2 41.8 %reduce-scatter.4.cloned.1.call-done = f32[1408,64]{0,1:T(8,128)} async-done(((f32[1408,512]{0,1:T(8,128)}), f32[1408,64]{0,1:T(8,128)}) %reduce-scatter.4.cloned.1.call-update) | async-done | bytes 360464 | tf_op jit(solution)/shard_map/reduce_scatter | solution.py:33
  54.9 0.0 all-gather.4.cloned.1.call-update
  55.0 0.0 all-gather.6.cloned.1.call-start
  55.0 0.0 copy-done.4
  55.0 0.1 copy.20
  55.1 0.1 reduce-window.8
  55.2 0.1 add_reduce_fusion
  55.3 30.5 %all-gather.4.cloned.1.call-done = f32[5632,64]{0,1:T(8,128)} async-done(((f32[1408,64]{0,1:T(8,128)}), f32[5632,64]{0,1:T(8,128)}) %all-gather.4.cloned.1.call-update) | async-done | bytes 1441808 | tf_op jit(solution)/shard_map/all_gather | solution.py:34
  85.8 1.5 reshape.103
  87.3 0.6 fusion.7
  87.9 0.9 copy.33
  88.8 0.0 all-gather.6.cloned.1.call-update
  88.8 0.0 all-gather.8.cloned.1.call-start
  88.9 0.1 convert_reduce_fusion
  89.0 38.2 %all-gather.6.cloned.1.call-done = f32[1536,512]{0,1:T(8,128)} async-done(((f32[1536,64]{0,1:T(8,128)}), f32[1536,512]{0,1:T(8,128)}) %all-gather.6.cloned.1.call-update) | async-done | bytes 3145744 | tf_op jit(solution)/shard_map/all_gather | solution.py:49
  127.2 2.4 copy.24
  129.6 4.0 %fusion.2 = f32[12,128,512]{2,0,1:T(8,128)S(1)} fusion(f32[12,128,512]{2,1,0:T(8,128)S(1)} %bitcast.36, pred[]{:T(512)S(6)} %eq.41, s32[12]{0:T(128)S(1)} %get-tuple-element.6, s32[12]{0:T(128)S(1)} %get-tuple-element.7), kind=kOutput, calls=%fused_computation.5 | convolution fusion | flops 114032784 | bytes 6291553 | tf_op jit(solution)/shard_map/kp,pbw->kbw/dot_general | solution.py:16
  133.6 3.4 copy.26
  137.1 0.0 all-gather.8.cloned.1.call-update
  137.1 0.0 reduce-scatter.6.cloned.1.call-start
  137.1 19.2 %copy.21 = f32[1536,3072]{0,1:T(8,128)} copy(f32[1536,3072]{1,0:T(8,128)} %param.5) | data formatting | bytes 37748736 | tf_op args[0]
  156.4 18.6 %copy.22 = f32[1536,24,128]{2,0,1:T(8,128)} copy(f32[1536,24,128]{0,2,1:T(8,128)} %bitcast.34) | data formatting | bytes 37748736 | tf_op jit(solution)/shard_map/reshape | solution.py:50
  175.0 11.2 %gather_fusion = f32[12,1536,128]{2,1,0:T(8,128)} fusion(f32[1536,24,128]{2,0,1:T(8,128)} %copy.22, s32[1024]{0:T(1024)S(1)} %pad_clamp_fusion), kind=kCustom, calls=%fused_computation | custom fusion | bytes 18874416 | tf_op jit(solution)/shard_map/jit(_take)/gather | solution.py:50
  186.3 9.9 %copy.23 = f32[1536,12,128]{0,2,1:T(8,128)} copy(f32[1536,12,128]{2,0,1:T(8,128)} %bitcast.35) | data formatting | bytes 18874368 | tf_op jit(solution)/shard_map/jit(_take)/gather | solution.py:50
  196.2 0.1 broadcast_bitcast_fusion
  196.3 0.0 copy-start.2
  196.3 4.5 %bitcast_select_fusion = f32[1536,1536]{0,1:T(8,128)S(1)} fusion(f32[1536,12,128]{0,2,1:T(8,128)} %copy.23, pred[1536]{0:T(1024)(128)(4,1)S(1)} %broadcast_bitcast_fusion), kind=kLoop, calls=%fused_computation.1 | loop fusion | flops 2359296 | bytes 18875904 | tf_op jit(solution)/shard_map/jit(_take)/select_n | solution.py:50
  200.8 0.0 copy-done.2
  200.8 17.1 %convolution_negate_fusion = f32[512,1536]{1,0:T(8,128)} fusion(f32[1536,512]{0,1:T(8,128)S(1)} %copy-done.2, f32[1536,1536]{0,1:T(8,128)S(1)} %bitcast_select_fusion), kind=kOutput, calls=%fused_computation.4 | convolution fusion | flops 14496301056 | bytes 15728640 | tf_op jit(solution)/shard_map/dot_general | solution.py:53
  217.9 0.0 reduce-scatter.6.cloned.1.call-update
  217.9 0.0 reduce-scatter.8.cloned.1.call-start
  218.0 40.5 %all-gather.8.cloned.1.call-done = f32[4,1536,512]{2,1,0:T(8,128)} async-done(((f32[1,1536,512]{2,1,0:T(8,128)}), f32[4,1536,512]{2,1,0:T(8,128)}) %all-gather.8.cloned.1.call-update) | async-done | bytes 12582928 | tf_op jit(solution)/shard_map/all_gather | solution.py:11
  258.5 6.5 %reduce_sum.29 = f32[1536,512]{1,0:T(8,128)S(1)} reduce(f32[4,1536,512]{2,1,0:T(8,128)} %all-gather.8.cloned.1.call-done, f32[]{:T(128)} %constant.52.clone.1), dimensions={0}, to_apply=%region_5.6 | reduce | flops 2359296 | bytes 15728644 | tf_op jit(solution)/shard_map/reduce_sum | solution.py:11
  265.1 0.0 copy-start.3
  265.1 40.8 %reduce-scatter.6.cloned.1.call-done = f32[128,1536]{1,0:T(8,128)} async-done(((f32[512,1536]{1,0:T(8,128)}), f32[128,1536]{1,0:T(8,128)}) %reduce-scatter.6.cloned.1.call-update) | async-done | bytes 786448 | tf_op jit(solution)/shard_map/reduce_scatter | solution.py:52
  305.9 6.9 %convolution_negate_fusion.1 = f32[512,128]{1,0:T(8,128)} fusion(f32[1536,512]{1,0:T(8,128)S(1)} %reduce_sum.29, f32[128,1536]{1,0:T(8,128)} %reduce-scatter.6.cloned.1.call-done), kind=kOutput, calls=%fused_computation.6 | convolution fusion | flops 1208025088 | bytes 4194304 | tf_op jit(solution)/shard_map/dot_general | solution.py:69
  312.7 0.0 reduce-scatter.8.cloned.1.call-update
  312.8 31.0 %reduce-scatter.8.cloned.1.call-done = f32[64,128]{1,0:T(8,128)} async-done(((f32[512,128]{1,0:T(8,128)}), f32[64,128]{1,0:T(8,128)}) %reduce-scatter.8.cloned.1.call-update) | async-done | bytes 32784 | tf_op jit(solution)/shard_map/reduce_scatter | solution.py:76
  343.8 0.0 copy-done.3
  343.8 1.4 add.49
  345.1 0.0 copy-done.1
  (6 shorter events, 0.0 us)
Async XLA Ops:
  7.2 1.0 copy-start
  7.2 47.8 %copy-start.4 = (s32[44]{0:T(128)S(1)}, s32[44]{0:T(128)}, u32[]{:S(2)}) copy-start(s32[44]{0:T(128)} %param.9) | copy-start | bytes 532
  7.2 47.8 %reduce-scatter.4.cloned.1.call-start = ((), (), s32[]{:S(2)}) async-start(), calls=%async_computation.3 | async-start | bytes 3244032 | tf_op jit(solution)/shard_map/reduce_scatter | solution.py:33
  13.1 72.7 %all-gather.4.cloned.1.call-start = ((), (), s32[]{:S(2)}) async-start(), calls=%async_computation.4 | async-start | bytes 1802240 | tf_op jit(solution)/shard_map/all_gather | solution.py:34
  55.0 72.2 %all-gather.6.cloned.1.call-start = ((), (), s32[]{:S(2)}) async-start(), calls=%async_computation.5 | async-start | bytes 3538944 | tf_op jit(solution)/shard_map/all_gather | solution.py:49
  88.8 169.7 %all-gather.8.cloned.1.call-start = ((), (), s32[]{:S(2)}) async-start(), calls=%async_computation.7 | async-start | bytes 15728640 | tf_op jit(solution)/shard_map/all_gather | solution.py:11
  137.1 168.8 %reduce-scatter.6.cloned.1.call-start = ((), (), s32[]{:S(2)}) async-start(), calls=%async_computation.6 | async-start | bytes 3932160 | tf_op jit(solution)/shard_map/reduce_scatter | solution.py:52
  196.3 4.6 %copy-start.2 = (f32[1536,512]{0,1:T(8,128)S(1)}, f32[1536,512]{0,1:T(8,128)}, u32[]{:S(2)}) copy-start(f32[1536,512]{0,1:T(8,128)} %all-gather.6.cloned.1.call-done) | copy-start | bytes 9437188
  217.9 125.8 %reduce-scatter.8.cloned.1.call-start = ((), (), s32[]{:S(2)}) async-start(), calls=%async_computation.8 | async-start | bytes 294912 | tf_op jit(solution)/shard_map/reduce_scatter | solution.py:76
  258.5 86.6 %copy-start.1 = (f32[1408,64]{0,1:T(8,128)S(1)}, f32[1408,64]{0,1:T(8,128)}, u32[]{:S(2)}) copy-start(f32[1408,64]{0,1:T(8,128)} %param.6) | copy-start | bytes 1081348
  265.1 78.7 %copy-start.3 = (f32[64,128]{1,0:T(8,128)S(1)}, f32[64,128]{1,0:T(8,128)}, u32[]{:S(2)}) copy-start(f32[64,128]{1,0:T(8,128)} %param.8) | copy-start | bytes 98308
Sparse Core Ops, SparseCore 0:
  13.2 41.6 reduce-scatter.3
  56.8 28.9 all-gather.3
  88.9 38.2 all-gather.5
  137.2 121.2 all-gather.7
  261.9 43.8 reduce-scatter.5
  312.9 30.8 reduce-scatter.7
